TPU v7x, 32 devices: a whole 2x2x4 slice. The times are simulated.
32 devices in a mesh: row: 8 (over y, x, core), col: 4 (over z).
Axes of the slice: x: 2, y: 2, z: 4, core: 2. Of those that a mesh axis runs over, the one named last changes fastest.
Arguments:
- acts: bfloat16 [512, 16384], P('row', 'col'), may hold values from -6 to 6
- grads: float32 [16384, 512], P('col', 'row'), may hold values from -24 to 24
Outputs:
- factor: float32 [16384, 16384], P('row', 'col')
- applied: float32 [16384, 512], P('row', 'col')
- solution: float32 [16384, 512], P('col', 'row')
All inputs are finite; a program needn't handle non-finite values.
Results may differ from a plain program's by a relative error of at most 0.0003.
Values may be sent and summed in bfloat16 or wider, within the bound.
No kernel may reach another device: no remote copies, remote signals or barrier semaphores. Data moves between devices by JAX's collectives and lax.ppermute only.
A program may use at most 128 MiB of HBM per device.

v0:
```python
import math
import jax
import jax.numpy as jnp
from jax import lax
from jax.sharding import PartitionSpec as P

damping = 1.0
highest = lax.Precision.HIGHEST


def from_root(value, axis, source):
    kept = jnp.where(lax.axis_index(axis) == source, value, 0).astype(value.dtype)
    return lax.psum(kept, axis)


def step_size(feature_count, token_count):
    return 1.0 / (damping + (1.0 + math.sqrt(feature_count / token_count)) ** 2)


def local(acts, grads):
    row_count = lax.axis_size("row")
    col_count = lax.axis_size("col")
    row_ratio = row_count // col_count
    row_index = lax.axis_index("row")
    col_index = lax.axis_index("col")
    outer_width = acts.shape[1]
    inner_width = outer_width // row_ratio
    token_count = acts.shape[0] * row_count
    omega_step = step_size(outer_width * col_count, token_count)
    row_offset = row_index % row_ratio * inner_width
    owner_col = row_index // row_ratio
    column_panel = lax.all_gather(acts, "row", axis=0, tiled=True)
    owned_slice = lax.dynamic_slice_in_dim(column_panel, row_offset, inner_width, 1)
    inner_panel = from_root(owned_slice, "col", owner_col)
    gram_sum = lax.dot_general(
        inner_panel, column_panel, (((0,), (0,)), ((), ())), preferred_element_type=jnp.float32
    )
    gram_tile = gram_sum / token_count
    is_owner = (col_index == owner_col).astype(jnp.float32)
    gathered = lax.all_gather(grads, "row", axis=1, tiled=True)
    mirror_rows = lax.dynamic_slice_in_dim(gathered, row_offset, inner_width, 0)
    partial_sum = jnp.dot(gram_tile, gathered, precision=highest) + damping * is_owner * mirror_rows
    full_applied = lax.psum(partial_sum, "col")
    share = full_applied.shape[1] // col_count
    applied = lax.dynamic_slice_in_dim(full_applied, col_index * share, share, 1)
    mirror_coef = omega_step**3 * damping - 3.0 * omega_step**2
    empty_block = jnp.zeros((outer_width, full_applied.shape[1]), jnp.float32)
    placed = lax.dynamic_update_slice_in_dim(
        empty_block, full_applied * (mirror_coef * is_owner), row_offset, 0
    )
    second_sum = (
        omega_step**3
        * lax.dot_general(
            gram_tile,
            full_applied,
            (((0,), (0,)), ((), ())),
            precision=highest,
            preferred_element_type=jnp.float32,
        )
        + placed
    )
    solution = 3.0 * omega_step * grads + lax.psum_scatter(
        second_sum, "row", scatter_dimension=1, tiled=True
    )
    return (gram_tile, applied, solution)


def solution(mesh):
    in_specs = (P("row", "col"), P("col", "row"))
    out_specs = (P("row", "col"), P("row", "col"), P("col", "row"))
    return jax.shard_map(local, mesh=mesh, in_specs=in_specs, out_specs=out_specs, check_vma=False)
```

profile of v0, /device:TPU:0, one launch (start us, length us, event | category | flops | bytes accessed | tf_op | source)
XLA Modules:
  0.0 583.2 jit_solution(10916674862800319205)
XLA Ops:
  7.2 0.0 all-gather.3.cloned.1.call-start
  7.2 0.7 all-gather.3.cloned.1.call-update
  7.9 0.0 all-reduce.3.cloned.1.call-start
  8.0 41.2 %all-gather.3.cloned.1.call-done = bf16[512,4096]{1,0:T(8,128)(2,1)} async-done(((bf16[64,4096]{1,0:T(8,128)(2,1)}), bf16[512,4096]{1,0:T(8,128)(2,1)}) %all-gather.3.cloned.1.call-update) | async-done | bytes 4194320 | tf_op jit(solution)/shard_map/all_gather | solution.py:32
  49.2 3.4 dynamic-slice_select_fusion
  52.6 0.0 all-reduce.3.cloned.1.call-update
  52.7 0.0 all-gather.5.cloned.1.call-start
  52.7 0.7 all-gather.5.cloned.1.call-update
  53.4 0.0 all-reduce.5.cloned.1.call-start
  53.5 85.5 %all-reduce.3.cloned.1.call-done = bf16[512,2048]{1,0:T(8,128)(2,1)} async-done(((bf16[512,2048]{1,0:T(8,128)(2,1)}), bf16[512,2048]{1,0:T(8,128)(2,1)}) %all-reduce.3.cloned.1.call-update) | async-done | bytes 2097168 | tf_op jit(solution)/shard_map/psum | solution.py:13
  139.0 18.8 %convolution_multiply_fusion = f32[2048,4096]{1,0:T(8,128)} fusion(bf16[512,2048]{1,0:T(8,128)(2,1)} %all-reduce.3.cloned.1.call-done, bf16[512,4096]{1,0:T(8,128)(2,1)} %all-gather.3.cloned.1.call-done), kind=kOutput, calls=%fused_computation | convolution fusion | flops 8598323200 | bytes 39845888 | tf_op jit(solution)/shard_map/dot_general | solution.py:35
  157.7 36.5 %all-gather.5.cloned.1.call-done = f32[4096,512]{0,1:T(8,128)} async-done(((f32[4096,64]{0,1:T(8,128)}), f32[4096,512]{0,1:T(8,128)}) %all-gather.5.cloned.1.call-update) | async-done | bytes 8388624 | tf_op jit(solution)/shard_map/all_gather | solution.py:40
  194.2 4.6 constant_dynamic-slice_fusion.1
  198.8 5.3 copy.13
  204.2 62.2 %multiply_add_fusion = f32[2048,512]{1,0:T(8,128)} fusion(f32[2048,512]{1,0:T(8,128)} %copy.13, f32[2048,4096]{1,0:T(8,128)} %convolution_multiply_fusion, f32[4096,512]{0,1:T(8,128)} %all-gather.5.cloned.1.call-done, f32[]{:T(128)S(6)} %convert_element_type.5), kind=kOutput, calls=%fused_computation.3 | convolution fusion | flops 51541704704 | bytes 50331652 | tf_op jit(solution)/shard_map/dot_general | solution.py:42
  266.3 0.0 all-reduce.5.cloned.1.call-update
  266.4 0.0 reduce-scatter.4.cloned.1.call-start
  266.4 155.1 %all-reduce.5.cloned.1.call-done = f32[2048,512]{1,0:T(8,128)} async-done(((f32[2048,512]{1,0:T(8,128)}), f32[2048,512]{1,0:T(8,128)}) %all-reduce.5.cloned.1.call-update) | async-done | bytes 4194320 | tf_op jit(solution)/shard_map/psum | solution.py:43
  421.5 0.0 copy-start
  421.5 60.8 %convolution_multiply_fusion.1 = f32[4096,512]{1,0:T(8,128)} fusion(f32[2048,4096]{1,0:T(8,128)} %convolution_multiply_fusion, f32[2048,512]{1,0:T(8,128)} %all-reduce.5.cloned.1.call-done), kind=kOutput, calls=%fused_computation.1 | convolution fusion | flops 51541704704 | bytes 46137344 | tf_op jit(solution)/shard_map/dot_general | solution.py:53
  482.3 0.0 copy-done
  482.3 5.2 add_dynamic-update-slice_fusion
  487.5 9.0 %copy.11 = f32[4096,512]{0,1:T(8,128)} copy(f32[4096,512]{1,0:T(8,128)} %add_dynamic-update-slice_fusion) | data formatting | bytes 16777216
  496.5 0.0 copy-start.1
  496.5 0.0 reduce-scatter.4.cloned.1.call-update
  496.5 1.2 copy-done.1
  497.7 0.6 copy.9
  498.3 2.3 constant_dynamic-slice_fusion
  500.6 66.6 %reduce-scatter.4.cloned.1.call-done = f32[64,4096]{1,0:T(8,128)} async-done(((f32[512,4096]{1,0:T(8,128)}), f32[64,4096]{1,0:T(8,128)}) %reduce-scatter.4.cloned.1.call-update) | async-done | bytes 1048592
  567.2 3.2 copy.12
  570.4 3.2 multiply_add_fusion.1
  573.5 3.1 copy.10
Async XLA Ops:
  7.2 42.0 %all-gather.3.cloned.1.call-start = ((), (), s32[]{:S(2)}) async-start(), calls=%async_computation.1 | async-start | bytes 4718592 | tf_op jit(solution)/shard_map/all_gather | solution.py:32
  7.9 131.1 %all-reduce.3.cloned.1.call-start = ((), (), s32[]{:S(2)}) async-start(), calls=%async_computation.2 | async-start | bytes 4194304 | tf_op jit(solution)/shard_map/psum | solution.py:13
  52.7 141.5 %all-gather.5.cloned.1.call-start = ((), (), s32[]{:S(2)}) async-start(), calls=%async_computation.3 | async-start | bytes 9437184 | tf_op jit(solution)/shard_map/all_gather | solution.py:40
  53.4 368.1 %all-reduce.5.cloned.1.call-start = ((), (), s32[]{:S(2)}) async-start(), calls=%async_computation.4 | async-start | bytes 8388608 | tf_op jit(solution)/shard_map/psum | solution.py:43
  266.4 300.8 %reduce-scatter.4.cloned.1.call-start = ((), (), s32[]{:S(2)}) async-start(), calls=%async_computation.5 | async-start | bytes 9437184
  421.5 60.8 %copy-start = (f32[2048,512]{1,0:T(8,128)S(1)}, f32[2048,512]{1,0:T(8,128)}, u32[]{:S(2)}) copy-start(f32[2048,512]{1,0:T(8,128)} %all-reduce.5.cloned.1.call-done) | copy-start | bytes 12582916
  496.5 1.2 copy-start.1
Sparse Core Ops, SparseCore 0:
  9.9 39.2 all-gather.2
  52.8 86.1 all-reduce.2
  140.9 53.2 all-gather.4
  266.5 154.9 all-reduce.4
  496.7 70.4 reduce-scatter.3
where the time goes:
time: 584 us; the launch traced here: 583 us
  waiting for transfers between devices  386 us (66%)
  matrix products  142 us (24%)
  local copies, waits for them, and re-layouts  29.4 us (5%)
  between operations  13.8 us (2%)
  other arithmetic  11.8 us (2%)
    psum x1, waiting for transfers between devices, local(): full_applied = lax.psum(partial_sum, 'col')  155 us
    psum x1, waiting for transfers between devices, from_root(): return lax.psum(kept, axis)  85.5 us
    unnamed x6, waiting for transfers between devices  68 us
    dot_general x1, matrix products, local(): jnp.dot(gram_tile, gathered, precision=highest)  62.2 us
    dot_general x1, matrix products, local(): lax.dot_general(gram_tile, full_applied, (((0,), (0,)), ((), ())), precis...  60.8 us
    all_gather x1, waiting for transfers between devices, local(): column_panel = lax.all_gather(acts, 'row', axis=0, tiled=True)  41.2 us
    all_gather x1, waiting for transfers between devices, local(): gathered = lax.all_gather(grads, 'row', axis=1, tiled=True)  36.5 us
    unnamed x9, local copies, waits for them, and re-layouts  22.5 us
  transfers between devices with their start and end apart: 5, of which 5 were waited for; matrix products, arithmetic and copies ran while one was open for 4% of the time, Pallas kernels for 0%

commit v1 on v0

--- a/solution.py
+++ b/solution.py
@@ -10,7 +10,7 @@
 
 def from_root(value, axis, source):
     kept = jnp.where(lax.axis_index(axis) == source, value, 0).astype(value.dtype)
-    return lax.psum(kept, axis)
+    return jnp.sum(lax.all_gather(kept, axis), axis=0)
 
 
 def step_size(feature_count, token_count):

time: 584 us -> 657 us (1.12)
  waiting for transfers between devices: 386 us -> 455 us
    all_gather x0 -> x1, waiting for transfers between devices: none -> 141 us  [from_root(): return jnp.sum(lax.all_gather(kept, axis), axis=0)]
    psum x1 -> x0, waiting for transfers between devices: 85.5 us -> none  [from_root(): return lax.psum(kept, axis)]
    all_gather x1, waiting for transfers between devices: 36.5 us -> 52.6 us  [local(): gathered = lax.all_gather(grads, 'row', axis=1, tiled=True)]
    unnamed x9 -> x11, local copies, waits for them, and re-layouts: 22.5 us -> 22.5 us
  transfers between devices with their start and end apart: 5 -> 5, of which waited for: 5 -> 5; matrix products, arithmetic and copies ran while one was open for 4% -> 3% of each run, Pallas kernels for 0% -> 0%
where the time goes in v1:
time: 657 us
  waiting for transfers between devices  455 us (69%)
  matrix products  140 us (21%)
  local copies, waits for them, and re-layouts  29.4 us (4%)
  other arithmetic  17.5 us (3%)
  between operations  13.9 us (2%)
    psum x1, waiting for transfers between devices, local(): full_applied = lax.psum(partial_sum, 'col')  153 us
    all_gather x1, waiting for transfers between devices, from_root(): return jnp.sum(lax.all_gather(kept, axis), axis=0)  141 us
    unnamed x6, waiting for transfers between devices  68 us
    dot_general x1, matrix products, local(): jnp.dot(gram_tile, gathered, precision=highest)  60.8 us
    dot_general x1, matrix products, local(): lax.dot_general(gram_tile, full_applied, (((0,), (0,)), ((), ())), precis...  60.8 us
    all_gather x1, waiting for transfers between devices, local(): gathered = lax.all_gather(grads, 'row', axis=1, tiled=True)  52.6 us
    all_gather x1, waiting for transfers between devices, local(): column_panel = lax.all_gather(acts, 'row', axis=0, tiled=True)  40.5 us
    unnamed x11, local copies, waits for them, and re-layouts  22.5 us
  transfers between devices with their start and end apart: 5, of which 5 were waited for; matrix products, arithmetic and copies ran while one was open for 3% of the time, Pallas kernels for 0%

profile of v1, /device:TPU:0, one launch (start us, length us, event | category | flops | bytes accessed | tf_op | source)
XLA Modules:
  0.0 656.7 jit_solution(17399756839932077292)
XLA Ops:
  7.2 0.0 all-gather.5.cloned.1.call-start
  7.2 0.7 all-gather.5.cloned.1.call-update
  7.9 0.0 all-gather.7.cloned.1.call-start
  7.9 0.7 all-gather.7.cloned.1.call-update
  8.6 0.0 all-gather.9.cloned.1.call-start
  8.7 40.5 %all-gather.5.cloned.1.call-done = bf16[512,4096]{1,0:T(8,128)(2,1)} async-done(((bf16[64,4096]{1,0:T(8,128)(2,1)}), bf16[512,4096]{1,0:T(8,128)(2,1)}) %all-gather.5.cloned.1.call-update) | async-done | bytes 4194320 | tf_op jit(solution)/shard_map/all_gather | solution.py:32
  49.2 3.5 dynamic-slice_select_fusion
  52.7 0.0 all-gather.9.cloned.1.call-update
  52.7 0.0 all-reduce.2.cloned.1.call-start
  52.8 52.6 %all-gather.7.cloned.1.call-done = f32[4096,512]{0,1:T(8,128)} async-done(((f32[4096,64]{0,1:T(8,128)}), f32[4096,512]{0,1:T(8,128)}) %all-gather.7.cloned.1.call-update) | async-done | bytes 8388624 | tf_op jit(solution)/shard_map/all_gather | solution.py:40
  105.4 4.7 constant_dynamic-slice_fusion.1
  110.1 5.4 copy.13
  115.5 141.1 %all-gather.9.cloned.1.call-done = bf16[2048,2048]{1,0:T(8,128)(2,1)} async-done(((bf16[512,2048]{1,0:T(8,128)(2,1)}), bf16[2048,2048]{1,0:T(8,128)(2,1)}) %all-gather.9.cloned.1.call-update) | async-done | bytes 8388624 | tf_op jit(solution)/shard_map/all_gather | solution.py:13
  256.6 5.7 reduce_sum.12
  262.3 0.0 copy-start.2
  262.3 18.6 %convolution_multiply_fusion = f32[2048,4096]{1,0:T(8,128)} fusion(bf16[512,2048]{1,0:T(8,128)(2,1)S(1)} %reduce_sum.12, bf16[512,4096]{1,0:T(8,128)(2,1)} %all-gather.5.cloned.1.call-done), kind=kOutput, calls=%fused_computation | convolution fusion | flops 8598323200 | bytes 39845888 | tf_op jit(solution)/shard_map/dot_general | solution.py:35
  280.9 0.0 copy-done.2
  280.9 60.8 %multiply_add_fusion = f32[2048,512]{1,0:T(8,128)} fusion(f32[2048,512]{1,0:T(8,128)S(1)} %copy-done.2, f32[2048,4096]{1,0:T(8,128)} %convolution_multiply_fusion, f32[4096,512]{0,1:T(8,128)} %all-gather.7.cloned.1.call-done, f32[]{:T(128)S(6)} %convert_element_type.4), kind=kOutput, calls=%fused_computation.3 | convolution fusion | flops 51541704704 | bytes 50331652 | tf_op jit(solution)/shard_map/dot_general | solution.py:42
  341.7 0.0 all-reduce.2.cloned.1.call-update
  341.8 0.0 reduce-scatter.4.cloned.1.call-start
  341.8 153.3 %all-reduce.2.cloned.1.call-done = f32[2048,512]{1,0:T(8,128)} async-done(((f32[2048,512]{1,0:T(8,128)}), f32[2048,512]{1,0:T(8,128)}) %all-reduce.2.cloned.1.call-update) | async-done | bytes 4194320 | tf_op jit(solution)/shard_map/psum | solution.py:43
  495.1 0.0 copy-start
  495.1 60.8 %convolution_multiply_fusion.1 = f32[4096,512]{1,0:T(8,128)} fusion(f32[2048,4096]{1,0:T(8,128)} %convolution_multiply_fusion, f32[2048,512]{1,0:T(8,128)} %all-reduce.2.cloned.1.call-done), kind=kOutput, calls=%fused_computation.1 | convolution fusion | flops 51541704704 | bytes 46137344 | tf_op jit(solution)/shard_map/dot_general | solution.py:53
  555.9 0.0 copy-done
  555.9 5.2 add_dynamic-update-slice_fusion
  561.1 8.9 %copy.11 = f32[4096,512]{0,1:T(8,128)} copy(f32[4096,512]{1,0:T(8,128)} %add_dynamic-update-slice_fusion) | data formatting | bytes 16777216
  570.0 0.0 copy-start.1
  570.0 0.0 reduce-scatter.4.cloned.1.call-update
  570.0 1.2 copy-done.1
  571.2 0.6 copy.9
  571.8 2.3 constant_dynamic-slice_fusion
  574.1 66.6 %reduce-scatter.4.cloned.1.call-done = f32[64,4096]{1,0:T(8,128)} async-done(((f32[512,4096]{1,0:T(8,128)}), f32[64,4096]{1,0:T(8,128)}) %reduce-scatter.4.cloned.1.call-update) | async-done | bytes 1048592
  640.7 3.2 copy.12
  643.9 3.2 multiply_add_fusion.1
  647.0 3.1 copy.10
Async XLA Ops:
  7.2 42.0 %all-gather.5.cloned.1.call-start = ((), (), s32[]{:S(2)}) async-start(), calls=%async_computation.1 | async-start | bytes 4718592 | tf_op jit(solution)/shard_map/all_gather | solution.py:32
  7.9 97.5 %all-gather.7.cloned.1.call-start = ((), (), s32[]{:S(2)}) async-start(), calls=%async_computation.2 | async-start | bytes 9437184 | tf_op jit(solution)/shard_map/all_gather | solution.py:40
  8.6 247.9 %all-gather.9.cloned.1.call-start = ((), (), s32[]{:S(2)}) async-start(), calls=%async_computation.4 | async-start | bytes 10485760 | tf_op jit(solution)/shard_map/all_gather | solution.py:13
  52.7 442.4 %all-reduce.2.cloned.1.call-start = ((), (), s32[]{:S(2)}) async-start(), calls=%async_computation.3 | async-start | bytes 8388608 | tf_op jit(solution)/shard_map/psum | solution.py:43
  262.3 18.6 %copy-start.2 = (f32[2048,512]{1,0:T(8,128)S(1)}, f32[2048,512]{1,0:T(8,128)}, u32[]{:S(2)}) copy-start(f32[2048,512]{1,0:T(8,128)} %copy.13) | copy-start | bytes 12582916
  341.8 298.9 %reduce-scatter.4.cloned.1.call-start = ((), (), s32[]{:S(2)}) async-start(), calls=%async_computation.5 | async-start | bytes 9437184
  495.1 60.8 %copy-start = (f32[2048,512]{1,0:T(8,128)S(1)}, f32[2048,512]{1,0:T(8,128)}, u32[]{:S(2)}) copy-start(f32[2048,512]{1,0:T(8,128)} %all-reduce.2.cloned.1.call-done) | copy-start | bytes 12582916
  570.0 1.2 copy-start.1
Sparse Core Ops, SparseCore 0:
  9.9 39.2 all-gather.4
  51.1 54.2 all-gather.6
  107.0 149.5 all-gather.8
  341.9 153.1 all-reduce.1
  570.2 70.4 reduce-scatter.3
